TPU v7x, 32 devices: a whole 2x2x4 slice. The times are simulated.
32 devices in a mesh: band: 4 (over y, core), tile: 8 (over z, x).
Axes of the slice: x: 2, y: 2, z: 4, core: 2. Of those that a mesh axis runs over, the one named last changes fastest.
Arguments:
- patches: bfloat16 [262144, 128], P(('band', 'tile')), may hold values from -6 to 6
- pair_patch: int32 [4096], P(('band', 'tile')), may hold values from 0 to 63
- pair_atm: int32 [4096], P(('band', 'tile')), may hold values from 0 to 4095, as said below
- numerators: int32 [4096, 128, 32], P(('band', 'tile')), may hold values from 0 to 16777215
- counts: int32 [32], P(('band', 'tile')), may hold values from 32 to 128, as said below
Outputs:
- atmosphere: float32 [131072, 128], P(('band', 'tile'))
Inputs may be any that keep to these rules, and one draw needn't show every extreme that they name: Block pair_atm[g] is owned by device pair_atm[g] // 128 (band-major device order). Every live pair of device (b, t) targets an owner in band b (any tile) or one of (b - 1, t), (b + 1, t). Among one device's live pairs at most 32 target one owner and at most 16 distinct blocks of one owner; both are reached on some device in every draw. Slots that are not live hold arbitrary blocks in range. `counts`: the value 128 occurs on some device in every draw.
All inputs are finite; a program needn't handle non-finite values.
Results may differ from a plain program's by a relative error of at most 0.0026.
Values sent between devices are 32-bit elements; how exact they have to be, the bound alone decides.
A program may use at most 64 MiB of HBM per device.

v0:
```python
import jax
import jax.numpy as jnp
from jax import lax
from jax.sharding import PartitionSpec as P

CELLS_DEV = 4096


SCALE = 2.0 ** (-27)


def shifted(value, axis, steps):
    count = lax.axis_size(axis)
    first, last = (max(0, -steps), min(count, count - steps))
    return lax.ppermute(value, axis, [(source, source + steps) for source in range(first, last)])


def slot_ranks(owners, blocks_local, live_pairs):
    position = jnp.arange(owners.shape[0])
    earlier = position[None, :] < position[:, None]
    both_live = live_pairs[None, :] & live_pairs[:, None]
    same_owner = (owners[:, None] == owners[None, :]) & both_live
    same_block = same_owner & (blocks_local[:, None] == blocks_local[None, :])
    leading = jnp.logical_not(jnp.any(same_block & earlier, axis=1))
    leader_rank = jnp.sum((same_owner & earlier & leading[None, :]).astype(jnp.int32), axis=1)
    first_match = same_block & leading[None, :]
    return jnp.sum(jnp.where(first_match, leader_rank[None, :], 0), axis=1)


def pack(flattened, rows_index, selected, blocks_local, rows_total):
    onehot = (rows_index[None, :] == jnp.arange(rows_total)[:, None]) & selected[None, :]
    payload = jnp.dot(onehot.astype(jnp.float32), flattened, precision=lax.Precision.HIGHEST)
    labels = jnp.max(jnp.where(onehot, blocks_local[None, :], -1), axis=1)
    return (payload, labels)


def unpack(payload, labels, blocks_owned):
    onehot = (labels[None, :] == jnp.arange(blocks_owned)[:, None]).astype(jnp.float32)
    return jnp.dot(onehot, payload, precision=lax.Precision.HIGHEST)


def along_band(parcel, offset_by):
    return shifted((parcel[0], parcel[1]), "band", offset_by)


def per_device(patches, pair_patch, pair_atm, numerators, counts):
    pairs_here, patch_rows, cell_rows = numerators.shape
    flux_width = patches.shape[1]
    blocks_owned = CELLS_DEV // cell_rows
    capacity = pairs_here // 4
    grouped = patches.reshape(-1, patch_rows, flux_width)
    live_pairs = jnp.arange(pairs_here) < counts[0]
    weight = (numerators.astype(jnp.float32) * SCALE).astype(jnp.bfloat16)
    chosen = grouped[pair_patch]
    partial_value = jnp.einsum("jpa,jpf->jaf", weight, chosen, preferred_element_type=jnp.float32)
    flattened = partial_value.reshape(pairs_here, cell_rows * flux_width)
    owners = pair_atm // blocks_owned
    blocks_local = pair_atm % blocks_owned
    slot_rank = slot_ranks(owners, blocks_local, live_pairs)
    bucket_size = capacity // 2
    tile_count = lax.axis_size("tile")
    band_now = lax.axis_index("band")
    tile_now = lax.axis_index("tile")
    owner_band = owners // tile_count
    owner_tile = owners % tile_count
    in_band = live_pairs & (owner_band == band_now)
    rows_index = jnp.where(in_band, owner_tile * bucket_size + slot_rank, -1)
    payload, labels = pack(flattened, rows_index, in_band, blocks_local, tile_count * bucket_size)

    def bucket(target):
        addressed = live_pairs & (owners == target)
        target_rows = jnp.where(addressed, slot_rank, -1)
        return pack(flattened, target_rows, addressed, blocks_local, bucket_size)

    upper_index = (band_now + 1) * tile_count + tile_now
    lower_index = (band_now - 1) * tile_count + tile_now
    from_below = along_band(bucket(upper_index), 1)
    from_above = along_band(bucket(lower_index), -1)
    band_payload = jnp.concatenate([from_below[0], from_above[0]], axis=0)
    band_labels = jnp.concatenate([from_below[1], from_above[1]], axis=0)
    payload, labels = (
        lax.all_to_all(
            payload.reshape(tile_count, bucket_size, -1),
            "tile",
            split_axis=0,
            concat_axis=0,
            tiled=True,
        ),
        lax.all_to_all(
            labels.reshape(tile_count, bucket_size), "tile", split_axis=0, concat_axis=0, tiled=True
        ),
    )
    payload = jnp.concatenate([payload.reshape(tile_count * bucket_size, -1), band_payload], axis=0)
    labels = jnp.concatenate([labels.reshape(-1), band_labels], axis=0)
    summed = unpack(payload, labels, blocks_owned)
    return summed.reshape(blocks_owned * cell_rows, flux_width)


def solution(mesh):
    placed = (
        P(("band", "tile"), None),
        P(("band", "tile")),
        P(("band", "tile")),
        P(("band", "tile"), None, None),
        P(("band", "tile")),
    )
    return jax.shard_map(
        per_device, mesh=mesh, in_specs=placed, out_specs=P(("band", "tile"), None), check_vma=False
    )
```

profile of v0, /device:TPU:0, one launch (start us, length us, event | category | flops | bytes accessed | tf_op | source)
XLA Modules:
  0.0 86.8 jit_solution(12213925503748507290)
XLA Ops:
  0.0 0.8 and_select_fusion
  1.5 0.2 fusion.17
  1.7 0.2 convert_reduce_fusion
  1.9 0.2 select_reduce_fusion.1
  2.2 0.7 all_to_all.9
  2.9 7.3 %all-to-all-start = ((s32[8,1,16]{2,1,0:T(1,128)}), s32[8,1,16]{2,1,0:T(1,128)S(1)}, u32[]{:S(2)}, u32[]{:S(2)}) async-start(s32[8,1,16]{2,1,0:T(1,128)} %bitcast.1), calls=%async_computation | async-start | bytes 8192 | tf_op jit(solution)/shard_map/all_to_all | solution.py:89
  10.2 0.7 compare_select_fusion
  10.9 3.0 %gather_fusion = bf16[128,128,128]{2,1,0:T(8,128)(2,1)} fusion(bf16[64,128,128]{2,1,0:T(8,128)(2,1)S(1)} %bitcast.14, s32[1024]{0:T(1024)S(1)} %pad_clamp_fusion), kind=kCustom, calls=%fused_computation | custom fusion | bytes 8389120 | tf_op jit(solution)/shard_map/gather | solution.py:54
  13.9 5.3 %fusion.12 = f32[128,32,128]{2,1,0:T(8,128)} fusion(bf16[128,128,128]{2,1,0:T(8,128)(2,1)} %gather_fusion, s32[128,128,32]{1,2,0:T(8,128)} %param.8), kind=kOutput, calls=%fused_computation.14 | convolution fusion | flops 135790592 | bytes 8388608 | tf_op jit(solution)/shard_map/jpa,jpf->jaf/dot_general | solution.py:55
  19.2 2.7 %reshape.80 = f32[128,4096,1]{1,0,2:T(8,128)} reshape(f32[128,32,128]{2,1,0:T(8,128)} %fusion.12) | data formatting | bytes 4194304 | tf_op jit(solution)/shard_map/reshape | solution.py:56
  21.9 4.1 %fusion.20 = f32[8,16,4096]{2,1,0:T(8,128)} fusion(f32[128,4096,1]{1,0,2:T(8,128)} %reshape.80, s32[8,16]{1,0:T(8,128)S(1)} %multiply_add_fusion, s32[128]{0:T(128)S(1)} %get-tuple-element.7, pred[128]{0:T(512)(128)(4,1)S(1)} %get-tuple-element.8), kind=kOutput, calls=%fused_computation.28 | convolution fusion | flops 805339136 | bytes 4195456 | tf_op jit(solution)/shard_map/dot_general | solution.py:32
  26.1 6.0 %all-to-all-start.1 = ((f32[8,16,4096]{2,1,0:T(8,128)}), f32[8,16,4096]{2,1,0:T(8,128)}, u32[]{:S(2)}, u32[]{:S(2)}) async-start(f32[8,16,4096]{2,1,0:T(8,128)} %fusion.20), calls=%async_computation.1 | async-start | bytes 4194304 | tf_op jit(solution)/shard_map/all_to_all | solution.py:82
  32.1 3.6 %fusion.8 = f32[16,4096]{1,0:T(8,128)S(1)} fusion(f32[16,8,32,128]{3,2,1,0:T(8,128)} %bitcast.15, s32[128]{0:T(128)S(1)} %get-tuple-element.13, pred[128]{0:T(512)(128)(4,1)S(1)} %get-tuple-element.14), kind=kOutput, calls=%fused_computation.9 | convolution fusion | flops 100667392 | bytes 2359936 | tf_op jit(solution)/shard_map/dot_general | solution.py:32
  35.7 1.3 %collective-permute-start.3 = (f32[16,4096]{1,0:T(8,128)S(1)}, f32[16,4096]{1,0:T(8,128)S(1)}, u32[]{:S(2)}, u32[]{:S(2)}) collective-permute-start(f32[16,4096]{1,0:T(8,128)S(1)} %fusion.8), channel_id=1, source_target_pairs={{8,0},{16,8},{24,16},{9,1},{17,9},{25,17},{10,2},{18,10},{26,18},{... | collective-permute-start | bytes 786440 | tf_op jit(solution)/shard_map/ppermute | solution.py:15
  37.0 2.0 %fusion.6 = f32[16,4096]{1,0:T(8,128)S(1)} fusion(f32[16,8,32,128]{3,2,1,0:T(8,128)S(1)} %bitcast.16, s32[128]{0:T(128)S(1)} %get-tuple-element.15, pred[128]{0:T(512)(128)(4,1)S(1)} %get-tuple-element.16), kind=kOutput, calls=%fused_computation.7 | convolution fusion | flops 100667392 | bytes 2359936 | tf_op jit(solution)/shard_map/dot_general | solution.py:32
  39.0 3.0 %collective-permute-start.2 = (f32[16,4096]{1,0:T(8,128)S(1)}, f32[16,4096]{1,0:T(8,128)S(1)}, u32[]{:S(2)}, u32[]{:S(2)}) collective-permute-start(f32[16,4096]{1,0:T(8,128)S(1)} %fusion.6), channel_id=1, source_target_pairs={{0,8},{8,16},{16,24},{1,9},{9,17},{17,25},{2,10},{10,18},{18,26},{... | collective-permute-start | bytes 786440 | tf_op jit(solution)/shard_map/ppermute | solution.py:15
  42.0 0.1 select_reduce_fusion.3
  42.1 1.3 %collective-permute-start.1 = (s32[16]{0:T(128)S(1)}, s32[16]{0:T(128)S(1)}, u32[]{:S(2)}, u32[]{:S(2)}) collective-permute-start(s32[16]{0:T(128)S(1)} %get-tuple-element.6), channel_id=1, source_target_pairs={{8,0},{16,8},{24,16},{9,1},{17,9},{25,17},{10,2},{18,10},{26,18},{... | collective-permute-start | bytes 200 | tf_op jit(solution)/shard_map/ppermute | solution.py:15
  43.4 3.7 %collective-permute-start = (s32[16]{0:T(128)S(1)}, s32[16]{0:T(128)S(1)}, u32[]{:S(2)}, u32[]{:S(2)}) collective-permute-start(s32[16]{0:T(128)S(1)} %get-tuple-element.5), channel_id=1, source_target_pairs={{0,8},{8,16},{16,24},{1,9},{9,17},{17,25},{2,10},{10,18},{18,26},{... | collective-permute-start | bytes 200 | tf_op jit(solution)/shard_map/ppermute | solution.py:15
  47.1 0.5 broadcast.108
  47.6 0.7 reduce.3
  48.5 31.4 %all-to-all-done.1 = f32[8,16,4096]{2,1,0:T(8,128)} async-done(((f32[8,16,4096]{2,1,0:T(8,128)}), f32[8,16,4096]{2,1,0:T(8,128)}, u32[]{:S(2)}, u32[]{:S(2)}) %all-to-all-start.1) | async-done | bytes 2097184 | tf_op jit(solution)/shard_map/all_to_all | solution.py:82
  79.9 4.3 %fusion = f32[128,4096]{1,0:T(8,128)} fusion(f32[16,4096]{1,0:T(8,128)S(1)} %collective-permute-done.3, f32[16,4096]{1,0:T(8,128)S(1)} %collective-permute-done.2, f32[128,4096]{1,0:T(8,128)} %bitcast.3, s32[160]{0:T(256)S(1)} %pad_add_fusion), kind=kOutput, calls=%fused_computation.1 | convolution fusion | flops 1007964160 | bytes 4719232 | tf_op jit(solution)/shard_map/dot_general | solution.py:39
  84.1 2.7 %reshape.70 = f32[4096,128]{1,0:T(8,128)} reshape(f32[128,4096]{1,0:T(8,128)} %fusion) | data formatting | bytes 4194304 | tf_op jit(solution)/shard_map/reshape | solution.py:96
  (17 shorter events, 0.3 us)
Async XLA Ops:
  0.0 10.9 %copy-start = (bf16[8192,128]{1,0:T(8,128)(2,1)S(1)}, bf16[8192,128]{1,0:T(8,128)(2,1)}, u32[]{:S(2)}) copy-start(bf16[8192,128]{1,0:T(8,128)(2,1)} %param.5) | copy-start | bytes 6291460
  2.9 23.2 %all-to-all-start = ((s32[8,1,16]{2,1,0:T(1,128)}), s32[8,1,16]{2,1,0:T(1,128)S(1)}, u32[]{:S(2)}, u32[]{:S(2)}) async-start(s32[8,1,16]{2,1,0:T(1,128)} %bitcast.1), calls=%async_computation | async-start | bytes 8192 | tf_op jit(solution)/shard_map/all_to_all | solution.py:89
  26.1 53.8 %all-to-all-start.1 = ((f32[8,16,4096]{2,1,0:T(8,128)}), f32[8,16,4096]{2,1,0:T(8,128)}, u32[]{:S(2)}, u32[]{:S(2)}) async-start(f32[8,16,4096]{2,1,0:T(8,128)} %fusion.20), calls=%async_computation.1 | async-start | bytes 4194304 | tf_op jit(solution)/shard_map/all_to_all | solution.py:82
  32.1 4.9 %copy-start.1 = (f32[128,32,128]{2,1,0:T(8,128)S(1)}, f32[128,32,128]{2,1,0:T(8,128)}, u32[]{:S(2)}) copy-start(f32[128,32,128]{2,1,0:T(8,128)} %fusion.12) | copy-start | bytes 6291460
  35.7 12.8 %collective-permute-start.3 = (f32[16,4096]{1,0:T(8,128)S(1)}, f32[16,4096]{1,0:T(8,128)S(1)}, u32[]{:S(2)}, u32[]{:S(2)}) collective-permute-start(f32[16,4096]{1,0:T(8,128)S(1)} %fusion.8), channel_id=1, source_target_pairs={{8,0},{16,8},{24,16},{9,1},{17,9},{25,17},{10,2},{18,10},{26,18},{... | collective-permute-start | bytes 786440 | tf_op jit(solution)/shard_map/ppermute | solution.py:15
  39.0 9.5 %collective-permute-start.2 = (f32[16,4096]{1,0:T(8,128)S(1)}, f32[16,4096]{1,0:T(8,128)S(1)}, u32[]{:S(2)}, u32[]{:S(2)}) collective-permute-start(f32[16,4096]{1,0:T(8,128)S(1)} %fusion.6), channel_id=1, source_target_pairs={{0,8},{8,16},{16,24},{1,9},{9,17},{17,25},{2,10},{10,18},{18,26},{... | collective-permute-start | bytes 786440 | tf_op jit(solution)/shard_map/ppermute | solution.py:15
  42.1 6.2 %collective-permute-start.1 = (s32[16]{0:T(128)S(1)}, s32[16]{0:T(128)S(1)}, u32[]{:S(2)}, u32[]{:S(2)}) collective-permute-start(s32[16]{0:T(128)S(1)} %get-tuple-element.6), channel_id=1, source_target_pairs={{8,0},{16,8},{24,16},{9,1},{17,9},{25,17},{10,2},{18,10},{26,18},{... | collective-permute-start | bytes 200 | tf_op jit(solution)/shard_map/ppermute | solution.py:15
  43.4 4.9 %collective-permute-start = (s32[16]{0:T(128)S(1)}, s32[16]{0:T(128)S(1)}, u32[]{:S(2)}, u32[]{:S(2)}) collective-permute-start(s32[16]{0:T(128)S(1)} %get-tuple-element.5), channel_id=1, source_target_pairs={{0,8},{8,16},{16,24},{1,9},{9,17},{17,25},{2,10},{10,18},{18,26},{... | collective-permute-start | bytes 200 | tf_op jit(solution)/shard_map/ppermute | solution.py:15
where the time goes:
time: 87.3 us; the launch traced here: 86.8 us
  waiting for transfers between devices  31.4 us (36%)
  starting transfers between devices  22.6 us (26%)
  matrix products  19.3 us (22%)
  local copies, waits for them, and re-layouts  9.71 us (11%)
  other arithmetic  3.08 us (4%)
    all_to_all x1, waiting for transfers between devices, per_device(): lax.all_to_all(payload.reshape(tile_count, bucket_size, -1), 'tile', spli...  31.4 us
    dot_general x3, matrix products, pack(): jnp.dot(onehot.astype(jnp.float32), flattened, precision=lax.Precision.HI...  9.69 us
    ppermute x4, starting transfers between devices, shifted(): lax.ppermute(value, axis, [(source, source + steps) for source in range(f...  9.29 us
    all_to_all x1, starting transfers between devices, per_device(): lax.all_to_all(labels.reshape(tile_count, bucket_size), 'tile', split_axi...  7.28 us
    all_to_all x1, starting transfers between devices, per_device(): lax.all_to_all(payload.reshape(tile_count, bucket_size, -1), 'tile', spli...  5.99 us
    dot_general x1, matrix products, per_device(): jnp.einsum('jpa,jpf->jaf', weight, chosen, preferred_element_type=jnp.flo...  5.35 us
    dot_general x1, matrix products, unpack(): return jnp.dot(onehot, payload, precision=lax.Precision.HIGHEST)  4.28 us
    gather x1, local copies, waits for them, and re-layouts, per_device(): chosen = grouped[pair_patch]  3.01 us
  transfers between devices with their start and end apart: 6, of which 1 were waited for; matrix products, arithmetic and copies ran while one was open for 26% of the time, Pallas kernels for 0%

commit v1 on v0

v1 whole, which is shorter than its diff:
```python
import functools

import jax
import jax.numpy as jnp
from jax import lax
from jax.experimental import pallas as pl
from jax.experimental.pallas import tpu as pltpu
from jax.sharding import PartitionSpec as P

CELLS_DEV = 4096
SCALE = 2.0 ** (-27)
MESH = pl.DeviceIdType.MESH
LANES = 128


def partners(count):
    if count & (count - 1) == 0:
        return [lambda me, k=k: me ^ k for k in range(count - 1, 0, -1)]
    return [lambda me, k=k: lax.rem(me + k, count) for k in range(1, count)]


def pack_kernel(tiles, bucket, blocks_owned, chunk,
                patch_ref, atm_ref, counts_ref, patches_hbm, numer_hbm,
                send_ref, labels_ref,
                patches_v, numer_v, table, used, patch_sem, numer_sems):
    pairs = numer_v.shape[0]
    patch_rows = numer_v.shape[2]
    chunks = pairs // chunk
    buckets = tiles + 2
    patch_copy = pltpu.make_async_copy(patches_hbm, patches_v, patch_sem)
    patch_copy.start()
    copies = []
    for c in range(chunks):
        part = pl.ds(c * chunk, chunk)
        copy = pltpu.make_async_copy(numer_hbm.at[part], numer_v.at[part], numer_sems.at[c])
        copy.start()
        copies.append(copy)
    band = lax.axis_index("band")
    live = counts_ref[0]

    for b in range(buckets):
        used[b] = 0

        @pl.loop(0, blocks_owned, unroll=16)
        def _(i):
            table[b * blocks_owned + i] = -1

        for s in range(bucket):
            labels_ref[b, 0, s] = -1
    patch_copy.wait()
    for c in range(chunks):
        copies[c].wait()

        @pl.when(c * chunk < live)
        def _():
            for j in range(chunk):
                g = c * chunk + j
                is_live = g < live
                atm = atm_ref[g]
                owner = lax.div(atm, blocks_owned)
                block = lax.rem(atm, blocks_owned)
                owner_band = lax.div(owner, tiles)
                owner_tile = lax.rem(owner, tiles)
                b = jnp.where(owner_band == band, owner_tile,
                              jnp.where(owner_band > band, tiles, tiles + 1))
                entry = b * blocks_owned + block
                known = table[entry]
                fresh = known < 0
                new = used[b]
                rank = jnp.where(fresh, new, known)

                @pl.when(is_live)
                def _():
                    table[entry] = rank
                    used[b] = jnp.where(fresh, new + 1, new)
                    labels_ref[b, 0, rank] = block

                slot = jnp.where(is_live, b * bucket + rank, buckets * bucket)
                rows = pl.multiple_of(patch_ref[g] * patch_rows, patch_rows)
                weight = (numer_v[g].astype(jnp.float32) * SCALE).astype(jnp.bfloat16)
                part = jnp.dot(weight, patches_v[pl.ds(rows, patch_rows), :],
                               preferred_element_type=jnp.float32)
                before = send_ref[slot]
                send_ref[slot] = jnp.where(fresh, part, before + part)


def send_kernel(tiles, bands, bucket, send_ref, labels_ref, recv_ref, recv_labels_ref,
                data_send, data_recv, label_send, label_recv):
    band, tile = lax.axis_index("band"), lax.axis_index("tile")
    barrier = pltpu.get_barrier_semaphore()
    steps = partners(tiles)
    for step in steps:
        pl.semaphore_signal(barrier, inc=1, device_id=(band, step(tile)), device_id_type=MESH)

    @pl.when(band < bands - 1)
    def _():
        pl.semaphore_signal(barrier, inc=1, device_id=(band + 1, tile), device_id_type=MESH)

    @pl.when(band > 0)
    def _():
        pl.semaphore_signal(barrier, inc=1, device_id=(band - 1, tile), device_id_type=MESH)

    neighbours = jnp.where(band < bands - 1, 1, 0) + jnp.where(band > 0, 1, 0)
    pl.semaphore_wait(barrier, tiles - 1 + neighbours)

    def pair(source, place, device, sem):
        rows = pl.ds(source * bucket, bucket)
        landing = pl.ds(place * bucket, bucket)
        return (
            pltpu.make_async_remote_copy(
                src_ref=labels_ref.at[source], dst_ref=recv_labels_ref.at[place],
                send_sem=label_send.at[sem], recv_sem=label_recv.at[sem],
                device_id=device, device_id_type=MESH),
            pltpu.make_async_remote_copy(
                src_ref=send_ref.at[rows], dst_ref=recv_ref.at[landing],
                send_sem=data_send.at[sem], recv_sem=data_recv.at[sem],
                device_id=device, device_id_type=MESH),
        )

    inside = [pair(step(tile), tile, (band, step(tile)), k) for k, step in enumerate(steps)]
    upward = pair(tiles, tiles, (band + 1, tile), tiles - 1)
    downward = pair(tiles + 1, tiles + 1, (band - 1, tile), tiles)
    for copies in inside[:2]:
        for copy in copies:
            copy.start()

    @pl.when(band < bands - 1)
    def _():
        for copy in upward:
            copy.start()

    @pl.when(band > 0)
    def _():
        for copy in downward:
            copy.start()

    for copies in inside[2:]:
        for copy in copies:
            copy.start()
    for copies in inside:
        for copy in copies:
            copy.wait()

    @pl.when(band < bands - 1)
    def _():
        for up, down in zip(upward, downward):
            up.wait_send()
            down.wait_recv()

    @pl.when(band > 0)
    def _():
        for up, down in zip(upward, downward):
            down.wait_send()
            up.wait_recv()


def add_kernel(tiles, bands, bucket, labels_ref, recv_labels_ref, send_hbm, recv_hbm, out_ref,
               landed, sems):
    band, tile = lax.axis_index("band"), lax.axis_index("tile")
    buckets = tiles + 2

    def copy_of(b, ref):
        rows = pl.ds(b * bucket, bucket)
        return pltpu.make_async_copy(ref.at[rows], landed.at[rows], sems.at[b])

    for b in range(buckets):
        if b < tiles:
            @pl.when(tile == b)
            def _():
                copy_of(b, send_hbm).start()

            @pl.when(tile != b)
            def _():
                copy_of(b, recv_hbm).start()
        else:
            copy_of(b, recv_hbm).start()
    out_ref[...] = jnp.zeros_like(out_ref)
    for b in range(buckets):
        copy_of(b, recv_hbm).wait()
        if b == tiles:
            valid = band > 0
        elif b == tiles + 1:
            valid = band < bands - 1
        else:
            valid = True
        for s in range(bucket):
            label = recv_labels_ref[b, 0, s]
            if b < tiles:
                label = jnp.where(tile == b, labels_ref[b, 0, s], label)

            @pl.when((label >= 0) & valid)
            def _():
                out_ref[label] += landed[b * bucket + s]


def per_device(tiles, bands, patches, pair_patch, pair_atm, numerators, counts):
    pairs, patch_rows, cell_rows = numerators.shape
    flux = patches.shape[1]
    blocks_owned = CELLS_DEV // cell_rows
    bucket = pairs // 8
    buckets = tiles + 2
    chunk = 16
    smem = pl.BlockSpec(memory_space=pltpu.SMEM)
    vmem = pl.BlockSpec(memory_space=pltpu.VMEM)
    anywhere = pl.BlockSpec(memory_space=pl.ANY)
    labels_shape = jax.ShapeDtypeStruct((buckets, 1, LANES), jnp.int32)
    recv_shape = jax.ShapeDtypeStruct((buckets * bucket, cell_rows, flux), jnp.float32)
    send, labels = pl.pallas_call(
        functools.partial(pack_kernel, tiles, bucket, blocks_owned, chunk),
        out_shape=(jax.ShapeDtypeStruct((buckets * bucket + 1, cell_rows, flux), jnp.float32), labels_shape),
        in_specs=[smem, smem, smem, anywhere, anywhere],
        out_specs=(vmem, smem),
        scratch_shapes=[
            pltpu.VMEM(patches.shape, patches.dtype),
            pltpu.VMEM((pairs, cell_rows, patch_rows), jnp.int32),
            pltpu.SMEM((buckets * blocks_owned,), jnp.int32),
            pltpu.SMEM((buckets,), jnp.int32),
            pltpu.SemaphoreType.DMA,
            pltpu.SemaphoreType.DMA((pairs // chunk,)),
        ],
        name="pack",
    )(pair_patch, pair_atm, counts, patches, jnp.transpose(numerators, (0, 2, 1)))
    recv, recv_labels = pl.pallas_call(
        functools.partial(send_kernel, tiles, bands, bucket),
        out_shape=(recv_shape, labels_shape),
        in_specs=[anywhere, anywhere],
        out_specs=(anywhere, anywhere),
        scratch_shapes=[pltpu.SemaphoreType.DMA((tiles + 1,))] * 4,
        compiler_params=pltpu.CompilerParams(collective_id=0, has_side_effects=True),
        name="exchange",
    )(send, labels)
    out = pl.pallas_call(
        functools.partial(add_kernel, tiles, bands, bucket),
        out_shape=jax.ShapeDtypeStruct((blocks_owned, cell_rows, flux), jnp.float32),
        in_specs=[smem, smem, anywhere, anywhere],
        out_specs=vmem,
        scratch_shapes=[
            pltpu.VMEM(recv_shape.shape, jnp.float32),
            pltpu.SemaphoreType.DMA((buckets,)),
        ],
        name="add",
    )(labels, recv_labels, send, recv)
    return out.reshape(blocks_owned * cell_rows, flux)


def solution(mesh):
    spec = P(("band", "tile"))
    placed = (
        P(("band", "tile"), None),
        spec,
        spec,
        P(("band", "tile"), None, None),
        spec,
    )
    body = functools.partial(per_device, mesh.shape["tile"], mesh.shape["band"])
    return jax.shard_map(body, mesh=mesh, in_specs=placed, out_specs=P(("band", "tile"), None), check_vma=False)
```

time: 87.3 us -> 68.4 us (0.78)
  Pallas kernels: 0 us -> 67.6 us
  waiting for transfers between devices: 31.4 us -> 0 us
  starting transfers between devices: 22.6 us -> 0 us
  matrix products: 19.3 us -> 0 us
  local copies, waits for them, and re-layouts: 9.71 us -> 0 us
  other arithmetic: 3.08 us -> 0 us
    pallas_call x0 -> x3, Pallas kernels: none -> 67.6 us  [the longest x1 57.2 us: per_device(): pl.pallas_call(functools.partial(send_kernel, tiles, bands, bucket), out_...]
    all_to_all x2 -> x0, waiting for transfers between devices: 31.4 us -> none  [the longest x1 31.4 us: per_device(): lax.all_to_all(payload.reshape(tile_count, bucket_size, -1), 'tile', spli...]
    dot_general x5 -> x0, matrix products: 19.3 us -> none  [the longest x3 9.69 us: pack(): jnp.dot(onehot.astype(jnp.float32), flattened, precision=lax.Precision.HI...]
    all_to_all x2 -> x0, starting transfers between devices: 13.3 us -> none  [the longest x1 7.28 us: per_device(): lax.all_to_all(labels.reshape(tile_count, bucket_size), 'tile', split_axi...]
    ppermute x4 -> x0, starting transfers between devices: 9.29 us -> none  [shifted(): lax.ppermute(value, axis, [(source, source + steps) for source in range(f...]
    reshape x3 -> x0, local copies, waits for them, and re-layouts: 5.49 us -> none  [the longest x1 2.71 us: per_device(): flattened = partial_value.reshape(pairs_here, cell_rows * flux_width)]
    gather x1 -> x0, local copies, waits for them, and re-layouts: 3.01 us -> none  [per_device(): chosen = grouped[pair_patch]]
    select_n x3 -> x0, other arithmetic: 1.49 us -> none  [the longest x1 0.81 us: per_device(): blocks_local = pair_atm % blocks_owned]
  transfers between devices with their start and end apart: 6 -> 0, of which waited for: 1 -> 0; matrix products, arithmetic and copies ran while one was open for 26% -> 0% of each run, Pallas kernels for 0% -> 0%
where the time goes in v1:
time: 68.4 us; the launch traced here: 68.2 us
  Pallas kernels  67.6 us (99%)
    pallas_call x1, Pallas kernels, per_device(): pl.pallas_call(functools.partial(send_kernel, tiles, bands, bucket), out_...  57.2 us
    pallas_call x1, Pallas kernels, per_device(): pl.pallas_call(functools.partial(pack_kernel, tiles, bucket, blocks_owned...  5.7 us
    pallas_call x1, Pallas kernels, per_device(): pl.pallas_call(functools.partial(add_kernel, tiles, bands, bucket), out_s...  4.61 us

profile of v1, /device:TPU:0, one launch (start us, length us, event | category | flops | bytes accessed | tf_op | source)
XLA Modules:
  0.0 68.2 jit_solution(8009176167546438063)
XLA Ops:
  0.7 5.7 %pack.1 = (f32[161,32,128]{2,1,0:T(8,128)}, s32[10,1,128]{2,1,0:T(1,128)}) custom-call(s32[128]{0:T(128)} %patch_ref.1, s32[128]{0:T(128)} %atm_ref.1, s32[1]{0:T(128)S(6)} %copy.6.counts_ref, bf16[8192,128]{1,0:T(8,128)(2,1)} %patches_hbm.1, s32[128,32,128]{2,1,0:T(8,128)} %bitcast.2), custom_call_target="tpu_custom_call" | custom-call | tf_op jit(solution)/shard_map/pack/pallas_call | solution.py:208
  6.4 57.2 %exchange.1 = (f32[160,32,128]{2,1,0:T(8,128)}, s32[10,1,128]{2,1,0:T(1,128)}) custom-call(f32[161,32,128]{2,1,0:T(8,128)} %get-tuple-element.10.send_ref.send_hbm, s32[10,1,128]{2,1,0:T(1,128)} %get-tuple-element.9.labels_ref), custom_call_target="tpu_custom_call" | custom-call | tf_op jit(solution)/shard_map/exchange/pallas_call | solution.py:223
  63.6 4.6 %add.1 = f32[128,32,128]{2,1,0:T(8,128)} custom-call(s32[10,1,128]{2,1,0:T(1,128)} %get-tuple-element.9.labels_ref, s32[10,1,128]{2,1,0:T(1,128)} %get-tuple-element.11.recv_labels_ref, f32[161,32,128]{2,1,0:T(8,128)} %get-tuple-element.10.send_ref.send_hbm, f32[160,32,128]{2,1,0:T(8,128)} %get-tuple-element.12.recv_hbm), custom_call_target="tpu_custom_call" | custom-call | tf_op jit(solution)/shard_map/add/pallas_call | solution.py:232

commit v2 on v1

--- a/solution.py
+++ b/solution.py
@@ -243,6 +243,333 @@
     return out.reshape(blocks_owned * cell_rows, flux)
 
 
+def ring_order(tiles):
+    wide = tiles // 4
+    if wide * 4 != tiles or wide % 2:
+        return list(range(tiles))
+    order = list(range(wide))
+    for step, column in enumerate(reversed(range(wide))):
+        rows = range(1, 4) if step % 2 == 0 else range(3, 0, -1)
+        order += [row * wide + column for row in rows]
+    return order
+
+
+def chosen(values, index):
+    picked = values[0]
+    for k in range(1, len(values)):
+        picked = jnp.where(index == k, values[k], picked)
+    return picked
+
+
+def ring_tile(tiles, tile, steps):
+    order = ring_order(tiles)
+    position = chosen([order.index(k) for k in range(tiles)], tile)
+    return chosen(order, lax.rem(position + steps + tiles, tiles))
+
+
+def list_kernel(tiles, bands, bucket, blocks_owned, chunk,
+                patch_ref, atm_ref, counts_ref, patches_hbm, numer_hbm,
+                send_ref, labels_ref,
+                patches_v, numer_v, table, used, patch_sem, numer_sems):
+    pairs = numer_v.shape[0]
+    patch_rows = numer_v.shape[2]
+    chunks = pairs // chunk
+    patch_copy = pltpu.make_async_copy(patches_hbm, patches_v, patch_sem)
+    patch_copy.start()
+    copies = []
+    for c in range(chunks):
+        part = pl.ds(c * chunk, chunk)
+        copy = pltpu.make_async_copy(numer_hbm.at[part], numer_v.at[part], numer_sems.at[c])
+        copy.start()
+        copies.append(copy)
+    band, tile = lax.axis_index("band"), lax.axis_index("tile")
+    live = counts_ref[0]
+    edge = (band == 0) | (band == bands - 1)
+    capacity = jnp.where(edge, 2 * bucket, bucket)
+
+    @pl.loop(0, (tiles + 2) * blocks_owned, step=16)
+    def _(i):
+        for j in range(16):
+            table[i + j] = -1
+
+    for b in range(4):
+        used[b] = 0
+    for s in range(5 * bucket):
+        labels_ref[0, s] = -1
+    labels_ref[0, LANES - 1] = 0
+    patch_copy.wait()
+    for c in range(chunks):
+        copies[c].wait()
+
+        @pl.when(c * chunk < live)
+        def _():
+            for j in range(chunk):
+                g = c * chunk + j
+                is_live = g < live
+                atm = atm_ref[g]
+                owner = lax.div(atm, blocks_owned)
+                block = lax.rem(atm, blocks_owned)
+                owner_band = lax.div(owner, tiles)
+                owner_tile = lax.rem(owner, tiles)
+                inside = owner_band == band
+                own = inside & (owner_tile == tile)
+                b = jnp.where(inside, owner_tile, jnp.where(owner_band > band, tiles, tiles + 1))
+                kind = jnp.where(own, 3, jnp.where(inside, 0, jnp.where(owner_band > band, 1, 2)))
+                base = jnp.where(kind == 0, 0, (kind + 1) * bucket)
+                entry = b * blocks_owned + block
+                known = table[entry]
+                fresh = known < 0
+                new = used[kind]
+                rank = jnp.where(fresh, new, known)
+                fits = is_live & ((kind > 0) | (rank < capacity))
+                slot = jnp.where(fits, base + rank, 5 * bucket)
+
+                @pl.when(is_live)
+                def _():
+                    table[entry] = rank
+                    used[kind] = jnp.where(fresh, new + 1, new)
+                    labels_ref[0, slot] = jnp.where(kind == 0, entry, block)
+
+                @pl.when(is_live & jnp.logical_not(fits))
+                def _():
+                    labels_ref[0, LANES - 1] = 1
+
+                rows = pl.multiple_of(patch_ref[g] * patch_rows, patch_rows)
+                weight = (numer_v[g].astype(jnp.float32) * SCALE).astype(jnp.bfloat16)
+                part = jnp.dot(weight, patches_v[pl.ds(rows, patch_rows), :],
+                               preferred_element_type=jnp.float32)
+                before = send_ref[slot]
+                send_ref[slot] = jnp.where(fresh, part, before + part)
+
+
+def ring_kernel(tiles, bands, bucket, send_ref, labels_ref, recv_ref, beside_ref, table_ref,
+                ring_send, ring_recv, beside_send, beside_recv, label_send, label_recv, local_sem):
+    band, tile = lax.axis_index("band"), lax.axis_index("tile")
+    steps = partners(tiles)
+    mine = pltpu.make_async_copy(labels_ref, table_ref.at[band, tile], local_sem)
+    mine.start()
+    barrier = pltpu.get_barrier_semaphore()
+    for step in steps:
+        pl.semaphore_signal(barrier, inc=1, device_id=(band, step(tile)), device_id_type=MESH)
+    for j in range(1, bands):
+        pl.semaphore_signal(barrier, inc=1, device_id=(lax.rem(band + j, bands), tile), device_id_type=MESH)
+    pl.semaphore_wait(barrier, tiles + bands - 2)
+
+    reach = tiles // 2
+    piece = bucket // 2
+    targets = ((band, ring_tile(tiles, tile, 1)), (band, ring_tile(tiles, tile, -1)))
+
+    def hop(way, distance, part):
+        rows = pl.ds(part * piece, piece)
+        source = send_ref.at[rows] if distance == 1 else recv_ref.at[way, distance - 2, rows]
+        return pltpu.make_async_remote_copy(
+            src_ref=source, dst_ref=recv_ref.at[way, distance - 1, rows],
+            send_sem=ring_send.at[way, distance - 1, part], recv_sem=ring_recv.at[way, distance - 1, part],
+            device_id=targets[way], device_id_type=MESH)
+
+    def beside(way, target_band):
+        return pltpu.make_async_remote_copy(
+            src_ref=send_ref.at[pl.ds((2 + way) * bucket, bucket)], dst_ref=beside_ref.at[way],
+            send_sem=beside_send.at[way], recv_sem=beside_recv.at[way],
+            device_id=(target_band, tile), device_id_type=MESH)
+
+    def travels(way, distance, part, parts):
+        return distance < reach or (part < parts // 2) == (way == 0)
+
+    is_edge = (band == 0) | (band == bands - 1)
+    for edge, parts in ((True, 4), (False, 2)):
+        @pl.when(is_edge if edge else jnp.logical_not(is_edge))
+        def _():
+            for part in range(parts):
+                for way in range(2):
+                    if travels(way, 1, part, parts):
+                        hop(way, 1, part).start()
+
+    upward, downward = beside(0, band + 1), beside(1, band - 1)
+
+    @pl.when(band < bands - 1)
+    def _():
+        upward.start()
+
+    @pl.when(band > 0)
+    def _():
+        downward.start()
+
+    inside = [
+        pltpu.make_async_remote_copy(
+            src_ref=labels_ref, dst_ref=table_ref.at[band, tile],
+            send_sem=label_send.at[k], recv_sem=label_recv.at[k],
+            device_id=(band, step(tile)), device_id_type=MESH)
+        for k, step in enumerate(steps)
+    ]
+    across = [
+        pltpu.make_async_remote_copy(
+            src_ref=table_ref.at[band], dst_ref=table_ref.at[band],
+            send_sem=label_send.at[tiles - 2 + j], recv_sem=label_recv.at[tiles - 2 + j],
+            device_id=(lax.rem(band + j, bands), tile), device_id_type=MESH)
+        for j in range(1, bands)
+    ]
+    for copy in inside:
+        copy.start()
+
+    for edge, parts in ((True, 4), (False, 2)):
+        @pl.when(is_edge if edge else jnp.logical_not(is_edge))
+        def _():
+            for distance in range(1, reach + 1):
+                for part in range(parts):
+                    for way in range(2):
+                        if not travels(way, distance, part, parts):
+                            continue
+                        hop(way, distance, part).wait_recv()
+                        if distance < reach and travels(way, distance + 1, part, parts):
+                            hop(way, distance + 1, part).start()
+                if distance == 1:
+                    mine.wait()
+                    for copy in inside:
+                        copy.wait()
+                    for copy in across:
+                        copy.start()
+            for distance in range(1, reach + 1):
+                for part in range(parts):
+                    for way in range(2):
+                        if travels(way, distance, part, parts):
+                            hop(way, distance, part).wait_send()
+    for copy in across:
+        copy.wait()
+
+    @pl.when(band < bands - 1)
+    def _():
+        upward.wait_send()
+        downward.wait_recv()
+
+    @pl.when(band > 0)
+    def _():
+        downward.wait_send()
+        upward.wait_recv()
+
+
+def take_kernel(tiles, bands, bucket, blocks_owned, labels_ref, table_ref, send_hbm, recv_hbm, beside_hbm, out_ref,
+                landed, beside, own, sems):
+    band, tile = lax.axis_index("band"), lax.axis_index("tile")
+    reach = tiles // 2
+    own_copy = pltpu.make_async_copy(send_hbm.at[pl.ds(4 * bucket, bucket)], own, sems.at[2 * reach])
+    beside_copy = pltpu.make_async_copy(beside_hbm, beside, sems.at[2 * reach + 1])
+    own_copy.start()
+    beside_copy.start()
+    copies = []
+    for distance in range(1, reach + 1):
+        for way in range(2):
+            copy = pltpu.make_async_copy(recv_hbm.at[way, distance - 1], landed.at[way, distance - 1],
+                                         sems.at[2 * (distance - 1) + way])
+            copy.start()
+            copies.append(copy)
+    out_ref[...] = jnp.zeros_like(out_ref)
+    own_copy.wait()
+    for s in range(bucket):
+        label = labels_ref[0, 4 * bucket + s]
+
+        @pl.when(label >= 0)
+        def _():
+            out_ref[label] += own[s]
+
+    beside_copy.wait()
+    for way in range(2):
+        other = jnp.clip(band - 1 if way == 0 else band + 1, 0, bands - 1)
+        valid = (band > 0) if way == 0 else (band < bands - 1)
+        for s in range(bucket):
+            label = table_ref[other, tile, 0, (2 + way) * bucket + s]
+
+            @pl.when((label >= 0) & valid)
+            def _():
+                out_ref[label] += beside[way, s]
+
+    half = jnp.where((band == 0) | (band == bands - 1), bucket, bucket // 2)
+    for distance in range(1, reach + 1):
+        for way in range(2):
+            copies[2 * (distance - 1) + way].wait()
+            source = ring_tile(tiles, tile, -distance if way == 0 else distance)
+            for s in range(2 * bucket):
+                label = table_ref[band, source, 0, s] - tile * blocks_owned
+                mine = (label >= 0) & (label < blocks_owned)
+                if distance == reach:
+                    mine = mine & ((s < half) if way == 0 else (s >= half))
+
+                @pl.when(mine)
+                def _():
+                    out_ref[label] += landed[way, distance - 1, s]
+
+
+def adaptive(tiles, bands, patches, pair_patch, pair_atm, numerators, counts):
+    pairs, patch_rows, cell_rows = numerators.shape
+    flux = patches.shape[1]
+    blocks_owned = CELLS_DEV // cell_rows
+    bucket = pairs // 8
+    reach = tiles // 2
+    chunk = 16
+    smem = pl.BlockSpec(memory_space=pltpu.SMEM)
+    vmem = pl.BlockSpec(memory_space=pltpu.VMEM)
+    anywhere = pl.BlockSpec(memory_space=pl.ANY)
+    block = (cell_rows, flux)
+    recv_shape = jax.ShapeDtypeStruct((2, reach, 2 * bucket) + block, jnp.float32)
+    beside_shape = jax.ShapeDtypeStruct((2, bucket) + block, jnp.float32)
+    send, labels = pl.pallas_call(
+        functools.partial(list_kernel, tiles, bands, bucket, blocks_owned, chunk),
+        out_shape=(jax.ShapeDtypeStruct((5 * bucket + 1,) + block, jnp.float32),
+                   jax.ShapeDtypeStruct((1, LANES), jnp.int32)),
+        in_specs=[smem, smem, smem, anywhere, anywhere],
+        out_specs=(vmem, smem),
+        scratch_shapes=[
+            pltpu.VMEM(patches.shape, patches.dtype),
+            pltpu.VMEM((pairs, cell_rows, patch_rows), jnp.int32),
+            pltpu.SMEM(((tiles + 2) * blocks_owned,), jnp.int32),
+            pltpu.SMEM((4,), jnp.int32),
+            pltpu.SemaphoreType.DMA,
+            pltpu.SemaphoreType.DMA((pairs // chunk,)),
+        ],
+        name="list",
+    )(pair_patch, pair_atm, counts, patches, jnp.transpose(numerators, (0, 2, 1)))
+    recv, beside, table = pl.pallas_call(
+        functools.partial(ring_kernel, tiles, bands, bucket),
+        out_shape=(recv_shape, beside_shape, jax.ShapeDtypeStruct((bands, tiles, 1, LANES), jnp.int32)),
+        in_specs=[anywhere, anywhere],
+        out_specs=(anywhere, anywhere, anywhere),
+        scratch_shapes=[
+            pltpu.SemaphoreType.DMA((2, reach, 4)),
+            pltpu.SemaphoreType.DMA((2, reach, 4)),
+            pltpu.SemaphoreType.DMA((2,)),
+            pltpu.SemaphoreType.DMA((2,)),
+            pltpu.SemaphoreType.DMA((tiles + bands - 2,)),
+            pltpu.SemaphoreType.DMA((tiles + bands - 2,)),
+            pltpu.SemaphoreType.DMA,
+        ],
+        compiler_params=pltpu.CompilerParams(collective_id=1, has_side_effects=True),
+        name="ring",
+    )(send, labels)
+
+    def take(patches, pair_patch, pair_atm, numerators, counts, labels, table, send, recv, beside):
+        out = pl.pallas_call(
+            functools.partial(take_kernel, tiles, bands, bucket, blocks_owned),
+            out_shape=jax.ShapeDtypeStruct((blocks_owned,) + block, jnp.float32),
+            in_specs=[smem, smem, anywhere, anywhere, anywhere],
+            out_specs=vmem,
+            scratch_shapes=[
+                pltpu.VMEM(recv_shape.shape, jnp.float32),
+                pltpu.VMEM(beside_shape.shape, jnp.float32),
+                pltpu.VMEM((bucket,) + block, jnp.float32),
+                pltpu.SemaphoreType.DMA((2 * reach + 2,)),
+            ],
+            name="take",
+        )(labels, table, send, recv, beside)
+        return out.reshape(blocks_owned * cell_rows, flux)
+
+    def padded(patches, pair_patch, pair_atm, numerators, counts, labels, table, send, recv, beside):
+        return per_device(tiles, bands, patches, pair_patch, pair_atm, numerators, counts)
+
+    overflowed = jnp.max(table[:, :, 0, LANES - 1]) > 0
+    return lax.cond(overflowed, padded, take, patches, pair_patch, pair_atm, numerators, counts,
+                    labels, table, send, recv, beside)
+
+
 def solution(mesh):
     spec = P(("band", "tile"))
     placed = (
@@ -252,5 +579,5 @@
         P(("band", "tile"), None, None),
         spec,
     )
-    body = functools.partial(per_device, mesh.shape["tile"], mesh.shape["band"])
+    body = functools.partial(adaptive, mesh.shape["tile"], mesh.shape["band"])
     return jax.shard_map(body, mesh=mesh, in_specs=placed, out_specs=P(("band", "tile"), None), check_vma=False)

time: 68.4 us -> 53 us (0.77)
  Pallas kernels: 67.6 us -> 49.1 us
  local copies, waits for them, and re-layouts: 0 us -> 1.33 us
  other arithmetic: 0 us -> 0.74 us
  between operations: 0.67 us -> 1.38 us
    pallas_call x3, Pallas kernels: 67.6 us -> 49.1 us  [the longest x1 38.8 us: adaptive(): pl.pallas_call(functools.partial(ring_kernel, tiles, bands, bucket), out_...]
    unnamed x0 -> x8, local copies, waits for them, and re-layouts: none -> 1.33 us
    reduce_max x0 -> x1, other arithmetic: none -> 0.74 us  [adaptive(): overflowed = jnp.max(table[:, :, 0, LANES - 1]) > 0]
where the time goes in v2:
time: 53 us; the launch traced here: 52.6 us
  Pallas kernels  49.1 us (93%)
  between operations  1.38 us (3%)
  local copies, waits for them, and re-layouts  1.33 us (3%)
  other arithmetic  0.74 us (1%)
    pallas_call x1, Pallas kernels, adaptive(): pl.pallas_call(functools.partial(ring_kernel, tiles, bands, bucket), out_...  38.8 us
    pallas_call x1, Pallas kernels, adaptive(): pl.pallas_call(functools.partial(list_kernel, tiles, bands, bucket, block...  5.81 us
    pallas_call x1, Pallas kernels, take(): pl.pallas_call(functools.partial(take_kernel, tiles, bands, bucket, block...  4.51 us
    unnamed x8, local copies, waits for them, and re-layouts  1.33 us

profile of v2, /device:TPU:0, one launch (start us, length us, event | category | flops | bytes accessed | tf_op | source)
XLA Modules:
  0.0 52.6 jit_solution(1929688579400233663)
XLA Ops:
  0.7 0.0 copy-start
  0.7 0.0 copy-start.2
  0.7 0.0 copy-start.3
  0.7 5.8 %list.1 = (f32[81,32,128]{2,1,0:T(8,128)S(1)}, s32[1,128]{1,0:T(1,128)S(1)}) custom-call(s32[128]{0:T(128)} %patch_ref.1, s32[128]{0:T(128)} %atm_ref.1, s32[1]{0:T(128)S(6)} %copy.10.counts_ref, bf16[8192,128]{1,0:T(8,128)(2,1)} %patches_hbm.1, s32[128,32,128]{2,1,0:T(8,128)} %bitcast.4), custom_call_target="tpu_custom_call" | custom-call | tf_op jit(solution)/shard_map/list/pallas_call | solution.py:515
  6.5 38.8 %ring.1 = (f32[2,4,32,32,128]{4,3,2,1,0:T(8,128)}, f32[2,16,32,128]{3,2,1,0:T(8,128)}, s32[4,8,1,128]{3,2,1,0:T(1,128)S(1)}) custom-call(f32[81,32,128]{2,1,0:T(8,128)S(1)} %get-tuple-element.47.send_ref, s32[1,128]{1,0:T(1,128)S(1)} %get-tuple-element.48.labels_ref), custom_call_target="tpu_custom_call" | custom-call | tf_op jit(solution)/shard_map/ring/pallas_call | solution.py:531
  45.3 0.7 %slice_reduce_fusion = s32[]{:T(128)} fusion(s32[4,8,1,128]{3,2,1,0:T(1,128)S(1)} %get-tuple-element.49), kind=kLoop, calls=%fused_computation | loop fusion | flops 31 | bytes 132 | tf_op jit(solution)/shard_map/reduce_max | solution.py:568
  46.7 0.0 copy-done
  46.7 0.0 copy-done.2
  46.7 0.0 copy-done.3
  46.7 4.5 %conditional.1 = (f32[4096,128]{1,0:T(8,128)S(1)}) conditional(s32[]{:T(128)} %convert_element_type.3, (s32[1,128]{1,0:T(1,128)S(1)}, s32[4,8,1,128]{3,2,1,0:T(1,128)S(1)}, f32[81,32,128]{2,1,0:T(8,128)S(1)}, f32[2,4,32,32,128]{4,3,2,1,0:T(8,128)}, f32[2,16,32,128]{3,2,1,0:T(8,128)}) %tuple.11, (s32[128,128,32]{1,2,0:T(8,128)}, s32[128]{0:T(128)S(1)}, ...), branch_computations={%region_1.0_spmd, %region_2.0_spmd} | conditional | bytes 8 | solution.py:569
  46.7 4.5 %take.1 = f32[128,32,128]{2,1,0:T(8,128)S(1)} custom-call(s32[1,128]{1,0:T(1,128)S(1)} %get-tuple-element.28.labels_ref, s32[4,8,1,128]{3,2,1,0:T(1,128)S(1)} %get-tuple-element.29.table_ref, f32[81,32,128]{2,1,0:T(8,128)S(1)} %get-tuple-element.30.send_hbm, f32[2,4,32,32,128]{4,3,2,1,0:T(8,128)} %get-tuple-element.31.recv_hbm, ...), custom_call_target="tpu_custom_call" | custom-call | tf_op jit(solution)/shard_map/cond/branch_0_fun/take/pallas_call | solution.py:550
  51.2 0.0 copy-start.1
  51.2 1.3 %copy-done.1 = f32[4096,128]{1,0:T(8,128)} copy-done((f32[4096,128]{1,0:T(8,128)}, f32[4096,128]{1,0:T(8,128)S(1)}, u32[]{:S(2)}) %copy-start.1) | copy-done | bytes 2097176
Async XLA Ops:
  0.7 46.0 %copy-start = (bf16[8192,128]{1,0:T(8,128)(2,1)S(1)}, bf16[8192,128]{1,0:T(8,128)(2,1)}, u32[]{:S(2)}) copy-start(bf16[8192,128]{1,0:T(8,128)(2,1)} %patches_hbm.1) | copy-start | bytes 6291460
  0.7 46.0 %copy-start.2 = (s32[128]{0:T(128)S(1)}, s32[128]{0:T(128)}, u32[]{:S(2)}) copy-start(s32[128]{0:T(128)} %patch_ref.1) | copy-start | bytes 1540
  0.7 46.0 %copy-start.3 = (s32[128]{0:T(128)S(1)}, s32[128]{0:T(128)}, u32[]{:S(2)}) copy-start(s32[128]{0:T(128)} %atm_ref.1) | copy-start | bytes 1540
  51.2 1.3 %copy-start.1 = (f32[4096,128]{1,0:T(8,128)}, f32[4096,128]{1,0:T(8,128)S(1)}, u32[]{:S(2)}) copy-start(f32[4096,128]{1,0:T(8,128)S(1)} %get-tuple-element.55) | copy-start | bytes 6291460

commit v3 on v2

--- a/solution.py
+++ b/solution.py
@@ -270,7 +270,7 @@
 def list_kernel(tiles, bands, bucket, blocks_owned, chunk,
                 patch_ref, atm_ref, counts_ref, patches_hbm, numer_hbm,
                 send_ref, labels_ref,
-                patches_v, numer_v, table, used, patch_sem, numer_sems):
+                patches_v, numer_v, table, used, slots, firsts, patch_sem, numer_sems):
     pairs = numer_v.shape[0]
     patch_rows = numer_v.shape[2]
     chunks = pairs // chunk
@@ -297,6 +297,38 @@
     for s in range(5 * bucket):
         labels_ref[0, s] = -1
     labels_ref[0, LANES - 1] = 0
+
+    @pl.loop(0, live)
+    def _(g):
+        atm = atm_ref[g]
+        owner = lax.div(atm, blocks_owned)
+        block = lax.rem(atm, blocks_owned)
+        owner_band = lax.div(owner, tiles)
+        owner_tile = lax.rem(owner, tiles)
+        inside = owner_band == band
+        own = inside & (owner_tile == tile)
+        b = jnp.where(inside, owner_tile, jnp.where(owner_band > band, tiles, tiles + 1))
+        kind = jnp.where(own, 3, jnp.where(inside, 0, jnp.where(owner_band > band, 1, 2)))
+        base = jnp.where(kind == 0, 0, (kind + 1) * bucket)
+        entry = b * blocks_owned + block
+        known = table[entry]
+        fresh = known < 0
+        new = used[kind]
+        rank = jnp.where(fresh, new, known)
+        fits = (kind > 0) | (rank < capacity)
+        slot = jnp.where(fits, base + rank, 5 * bucket)
+        table[entry] = rank
+        used[kind] = jnp.where(fresh, new + 1, new)
+        labels_ref[0, slot] = jnp.where(kind == 0, entry, block)
+        labels_ref[0, LANES - 1] = jnp.where(fits, labels_ref[0, LANES - 1], 1)
+        slots[g] = slot
+        firsts[g] = jnp.where(fresh, 1, 0)
+
+    @pl.loop(live, pairs)
+    def _(g):
+        slots[g] = 5 * bucket
+        firsts[g] = 1
+
     patch_copy.wait()
     for c in range(chunks):
         copies[c].wait()
@@ -305,41 +337,13 @@
         def _():
             for j in range(chunk):
                 g = c * chunk + j
-                is_live = g < live
-                atm = atm_ref[g]
-                owner = lax.div(atm, blocks_owned)
-                block = lax.rem(atm, blocks_owned)
-                owner_band = lax.div(owner, tiles)
-                owner_tile = lax.rem(owner, tiles)
-                inside = owner_band == band
-                own = inside & (owner_tile == tile)
-                b = jnp.where(inside, owner_tile, jnp.where(owner_band > band, tiles, tiles + 1))
-                kind = jnp.where(own, 3, jnp.where(inside, 0, jnp.where(owner_band > band, 1, 2)))
-                base = jnp.where(kind == 0, 0, (kind + 1) * bucket)
-                entry = b * blocks_owned + block
-                known = table[entry]
-                fresh = known < 0
-                new = used[kind]
-                rank = jnp.where(fresh, new, known)
-                fits = is_live & ((kind > 0) | (rank < capacity))
-                slot = jnp.where(fits, base + rank, 5 * bucket)
-
-                @pl.when(is_live)
-                def _():
-                    table[entry] = rank
-                    used[kind] = jnp.where(fresh, new + 1, new)
-                    labels_ref[0, slot] = jnp.where(kind == 0, entry, block)
-
-                @pl.when(is_live & jnp.logical_not(fits))
-                def _():
-                    labels_ref[0, LANES - 1] = 1
-
+                slot = slots[g]
                 rows = pl.multiple_of(patch_ref[g] * patch_rows, patch_rows)
                 weight = (numer_v[g].astype(jnp.float32) * SCALE).astype(jnp.bfloat16)
                 part = jnp.dot(weight, patches_v[pl.ds(rows, patch_rows), :],
                                preferred_element_type=jnp.float32)
                 before = send_ref[slot]
-                send_ref[slot] = jnp.where(fresh, part, before + part)
+                send_ref[slot] = jnp.where(firsts[g] == 1, part, before + part)
 
 
 def ring_kernel(tiles, bands, bucket, send_ref, labels_ref, recv_ref, beside_ref, table_ref,
@@ -449,20 +453,35 @@
 
 
 def take_kernel(tiles, bands, bucket, blocks_owned, labels_ref, table_ref, send_hbm, recv_hbm, beside_hbm, out_ref,
-                landed, beside, own, sems):
+                landed, beside, own, found_row, found_label, sems):
     band, tile = lax.axis_index("band"), lax.axis_index("tile")
     reach = tiles // 2
-    own_copy = pltpu.make_async_copy(send_hbm.at[pl.ds(4 * bucket, bucket)], own, sems.at[2 * reach])
-    beside_copy = pltpu.make_async_copy(beside_hbm, beside, sems.at[2 * reach + 1])
+    own_copy = pltpu.make_async_copy(send_hbm.at[pl.ds(4 * bucket, bucket)], own, sems.at[0])
+    beside_copy = pltpu.make_async_copy(beside_hbm, beside, sems.at[1])
     own_copy.start()
     beside_copy.start()
-    copies = []
-    for distance in range(1, reach + 1):
-        for way in range(2):
-            copy = pltpu.make_async_copy(recv_hbm.at[way, distance - 1], landed.at[way, distance - 1],
-                                         sems.at[2 * (distance - 1) + way])
-            copy.start()
-            copies.append(copy)
+
+    half = jnp.where((band == 0) | (band == bands - 1), bucket, bucket // 2)
+    found = jnp.int32(0)
+    for way in range(2):
+        for distance in range(1, reach + 1):
+            source = ring_tile(tiles, tile, -distance if way == 0 else distance)
+            for s in range(2 * bucket):
+                label = table_ref[band, source, 0, s] - tile * blocks_owned
+                mine = (label >= 0) & (label < blocks_owned)
+                if distance == reach:
+                    mine = mine & ((s < half) if way == 0 else (s >= half))
+                found_row[found] = (way * reach + distance - 1) * 2 * bucket + s
+                found_label[found] = label
+                found = found + jnp.where(mine, 1, 0)
+
+    def fetch(i):
+        return pltpu.make_async_copy(recv_hbm.at[found_row[i]], landed.at[i], sems.at[2])
+
+    @pl.loop(0, found)
+    def _(i):
+        fetch(i).start()
+
     out_ref[...] = jnp.zeros_like(out_ref)
     own_copy.wait()
     for s in range(bucket):
@@ -483,20 +502,13 @@
             def _():
                 out_ref[label] += beside[way, s]
 
-    half = jnp.where((band == 0) | (band == bands - 1), bucket, bucket // 2)
-    for distance in range(1, reach + 1):
-        for way in range(2):
-            copies[2 * (distance - 1) + way].wait()
-            source = ring_tile(tiles, tile, -distance if way == 0 else distance)
-            for s in range(2 * bucket):
-                label = table_ref[band, source, 0, s] - tile * blocks_owned
-                mine = (label >= 0) & (label < blocks_owned)
-                if distance == reach:
-                    mine = mine & ((s < half) if way == 0 else (s >= half))
-
-                @pl.when(mine)
-                def _():
-                    out_ref[label] += landed[way, distance - 1, s]
+    @pl.loop(0, found)
+    def _(i):
+        fetch(i).wait()
+
+    @pl.loop(0, found)
+    def _(i):
+        out_ref[found_label[i]] += landed[i]
 
 
 def adaptive(tiles, bands, patches, pair_patch, pair_atm, numerators, counts):
@@ -523,6 +535,8 @@
             pltpu.VMEM((pairs, cell_rows, patch_rows), jnp.int32),
             pltpu.SMEM(((tiles + 2) * blocks_owned,), jnp.int32),
             pltpu.SMEM((4,), jnp.int32),
+            pltpu.SMEM((pairs,), jnp.int32),
+            pltpu.SMEM((pairs,), jnp.int32),
             pltpu.SemaphoreType.DMA,
             pltpu.SemaphoreType.DMA((pairs // chunk,)),
         ],
@@ -553,13 +567,15 @@
             in_specs=[smem, smem, anywhere, anywhere, anywhere],
             out_specs=vmem,
             scratch_shapes=[
-                pltpu.VMEM(recv_shape.shape, jnp.float32),
+                pltpu.VMEM((4 * reach * bucket,) + block, jnp.float32),
                 pltpu.VMEM(beside_shape.shape, jnp.float32),
                 pltpu.VMEM((bucket,) + block, jnp.float32),
-                pltpu.SemaphoreType.DMA((2 * reach + 2,)),
+                pltpu.SMEM((4 * reach * bucket + 1,), jnp.int32),
+                pltpu.SMEM((4 * reach * bucket + 1,), jnp.int32),
+                pltpu.SemaphoreType.DMA((3,)),
             ],
             name="take",
-        )(labels, table, send, recv, beside)
+        )(labels, table, send, recv.reshape((4 * reach * bucket,) + block), beside)
         return out.reshape(blocks_owned * cell_rows, flux)
 
     def padded(patches, pair_patch, pair_atm, numerators, counts, labels, table, send, recv, beside):

time: 53 us -> 52.9 us (level)
    pallas_call x1, Pallas kernels: 38.8 us -> 40.5 us  [adaptive(): pl.pallas_call(functools.partial(ring_kernel, tiles, bands, bucket), out_...]
    pallas_call x1, Pallas kernels: 4.51 us -> 3.16 us  [take(): pl.pallas_call(functools.partial(take_kernel, tiles, bands, bucket, block...]
where the time goes in v3:
time: 52.9 us
  Pallas kernels  49.4 us (93%)
  between operations  1.38 us (3%)
  local copies, waits for them, and re-layouts  1.33 us (3%)
  other arithmetic  0.74 us (1%)
    pallas_call x1, Pallas kernels, adaptive(): pl.pallas_call(functools.partial(ring_kernel, tiles, bands, bucket), out_...  40.5 us
    pallas_call x1, Pallas kernels, adaptive(): pl.pallas_call(functools.partial(list_kernel, tiles, bands, bucket, block...  5.71 us
    pallas_call x1, Pallas kernels, take(): pl.pallas_call(functools.partial(take_kernel, tiles, bands, bucket, block...  3.16 us
    unnamed x8, local copies, waits for them, and re-layouts  1.33 us

profile of v3, /device:TPU:0, one launch (start us, length us, event | category | flops | bytes accessed | tf_op | source)
XLA Modules:
  0.0 52.9 jit_solution(13241721258822251875)
XLA Ops:
  0.7 0.0 copy-start
  0.7 0.0 copy-start.2
  0.7 0.0 copy-start.3
  0.7 5.7 %list.1 = (f32[81,32,128]{2,1,0:T(8,128)S(1)}, s32[1,128]{1,0:T(1,128)S(1)}) custom-call(s32[128]{0:T(128)} %patch_ref.1, s32[128]{0:T(128)} %atm_ref.1, s32[1]{0:T(128)S(6)} %copy.10.counts_ref, bf16[8192,128]{1,0:T(8,128)(2,1)} %patches_hbm.1, s32[128,32,128]{2,1,0:T(8,128)} %bitcast.5), custom_call_target="tpu_custom_call" | custom-call | tf_op jit(solution)/shard_map/list/pallas_call | solution.py:527
  6.4 40.5 %ring.1 = (f32[2,4,32,32,128]{4,3,2,1,0:T(8,128)}, f32[2,16,32,128]{3,2,1,0:T(8,128)}, s32[4,8,1,128]{3,2,1,0:T(1,128)S(1)}) custom-call(f32[81,32,128]{2,1,0:T(8,128)S(1)} %get-tuple-element.47.send_ref, s32[1,128]{1,0:T(1,128)S(1)} %get-tuple-element.48.labels_ref), custom_call_target="tpu_custom_call" | custom-call | tf_op jit(solution)/shard_map/ring/pallas_call | solution.py:545
  46.9 0.7 %slice_reduce_fusion = s32[]{:T(128)} fusion(s32[4,8,1,128]{3,2,1,0:T(1,128)S(1)} %get-tuple-element.49), kind=kLoop, calls=%fused_computation | loop fusion | flops 31 | bytes 132 | tf_op jit(solution)/shard_map/reduce_max | solution.py:584
  48.3 0.0 copy-done
  48.3 0.0 copy-done.2
  48.3 0.0 copy-done.3
  48.3 3.2 %conditional.1 = (f32[4096,128]{1,0:T(8,128)S(1)}) conditional(s32[]{:T(128)} %convert_element_type.3, (f32[2,4,32,32,128]{4,3,2,1,0:T(8,128)}, s32[1,128]{1,0:T(1,128)S(1)}, s32[4,8,1,128]{3,2,1,0:T(1,128)S(1)}, f32[81,32,128]{2,1,0:T(8,128)S(1)}, f32[2,16,32,128]{3,2,1,0:T(8,128)}) %tuple.11, (s32[128,128,32]{1,2,0:T(8,128)}, s32[128]{0:T(128)S(1)}, ...), branch_computations={%region_1.0_spmd, %region_2.0_spmd} | conditional | bytes 8 | solution.py:585
  48.4 3.2 %take.1 = f32[128,32,128]{2,1,0:T(8,128)S(1)} custom-call(s32[1,128]{1,0:T(1,128)S(1)} %get-tuple-element.28.labels_ref, s32[4,8,1,128]{3,2,1,0:T(1,128)S(1)} %get-tuple-element.29.table_ref, f32[81,32,128]{2,1,0:T(8,128)S(1)} %get-tuple-element.30.send_hbm, f32[256,32,128]{2,1,0:T(8,128)} %bitcast.7, f32[2,16,32,128]{3,2,1,0:T(8,128)} %get-tuple-element.32.beside_hbm), custom_call_target="tpu_custom_call" | custom-call | tf_op jit(solution)/shard_map/cond/branch_0_fun/take/pallas_call | solution.py:564
  51.5 0.0 copy-start.1
  51.5 1.3 %copy-done.1 = f32[4096,128]{1,0:T(8,128)} copy-done((f32[4096,128]{1,0:T(8,128)}, f32[4096,128]{1,0:T(8,128)S(1)}, u32[]{:S(2)}) %copy-start.1) | copy-done | bytes 2097176
Async XLA Ops:
  0.7 47.7 %copy-start = (bf16[8192,128]{1,0:T(8,128)(2,1)S(1)}, bf16[8192,128]{1,0:T(8,128)(2,1)}, u32[]{:S(2)}) copy-start(bf16[8192,128]{1,0:T(8,128)(2,1)} %patches_hbm.1) | copy-start | bytes 6291460
  0.7 47.7 %copy-start.2 = (s32[128]{0:T(128)S(1)}, s32[128]{0:T(128)}, u32[]{:S(2)}) copy-start(s32[128]{0:T(128)} %patch_ref.1) | copy-start | bytes 1540
  0.7 47.7 %copy-start.3 = (s32[128]{0:T(128)S(1)}, s32[128]{0:T(128)}, u32[]{:S(2)}) copy-start(s32[128]{0:T(128)} %atm_ref.1) | copy-start | bytes 1540
  51.5 1.3 %copy-start.1 = (f32[4096,128]{1,0:T(8,128)}, f32[4096,128]{1,0:T(8,128)S(1)}, u32[]{:S(2)}) copy-start(f32[4096,128]{1,0:T(8,128)S(1)} %get-tuple-element.55) | copy-start | bytes 6291460

commit v4 on v2

--- a/solution.py
+++ b/solution.py
@@ -449,20 +449,35 @@
 
 
 def take_kernel(tiles, bands, bucket, blocks_owned, labels_ref, table_ref, send_hbm, recv_hbm, beside_hbm, out_ref,
-                landed, beside, own, sems):
+                landed, beside, own, found_row, found_label, sems):
     band, tile = lax.axis_index("band"), lax.axis_index("tile")
     reach = tiles // 2
-    own_copy = pltpu.make_async_copy(send_hbm.at[pl.ds(4 * bucket, bucket)], own, sems.at[2 * reach])
-    beside_copy = pltpu.make_async_copy(beside_hbm, beside, sems.at[2 * reach + 1])
+    own_copy = pltpu.make_async_copy(send_hbm.at[pl.ds(4 * bucket, bucket)], own, sems.at[0])
+    beside_copy = pltpu.make_async_copy(beside_hbm, beside, sems.at[1])
     own_copy.start()
     beside_copy.start()
-    copies = []
-    for distance in range(1, reach + 1):
-        for way in range(2):
-            copy = pltpu.make_async_copy(recv_hbm.at[way, distance - 1], landed.at[way, distance - 1],
-                                         sems.at[2 * (distance - 1) + way])
-            copy.start()
-            copies.append(copy)
+
+    half = jnp.where((band == 0) | (band == bands - 1), bucket, bucket // 2)
+    found = jnp.int32(0)
+    for way in range(2):
+        for distance in range(1, reach + 1):
+            source = ring_tile(tiles, tile, -distance if way == 0 else distance)
+            for s in range(2 * bucket):
+                label = table_ref[band, source, 0, s] - tile * blocks_owned
+                mine = (label >= 0) & (label < blocks_owned)
+                if distance == reach:
+                    mine = mine & ((s < half) if way == 0 else (s >= half))
+                found_row[found] = (way * reach + distance - 1) * 2 * bucket + s
+                found_label[found] = label
+                found = found + jnp.where(mine, 1, 0)
+
+    def fetch(i):
+        return pltpu.make_async_copy(recv_hbm.at[found_row[i]], landed.at[i], sems.at[2])
+
+    @pl.loop(0, found)
+    def _(i):
+        fetch(i).start()
+
     out_ref[...] = jnp.zeros_like(out_ref)
     own_copy.wait()
     for s in range(bucket):
@@ -483,20 +498,13 @@
             def _():
                 out_ref[label] += beside[way, s]
 
-    half = jnp.where((band == 0) | (band == bands - 1), bucket, bucket // 2)
-    for distance in range(1, reach + 1):
-        for way in range(2):
-            copies[2 * (distance - 1) + way].wait()
-            source = ring_tile(tiles, tile, -distance if way == 0 else distance)
-            for s in range(2 * bucket):
-                label = table_ref[band, source, 0, s] - tile * blocks_owned
-                mine = (label >= 0) & (label < blocks_owned)
-                if distance == reach:
-                    mine = mine & ((s < half) if way == 0 else (s >= half))
-
-                @pl.when(mine)
-                def _():
-                    out_ref[label] += landed[way, distance - 1, s]
+    @pl.loop(0, found)
+    def _(i):
+        fetch(i).wait()
+
+    @pl.loop(0, found)
+    def _(i):
+        out_ref[found_label[i]] += landed[i]
 
 
 def adaptive(tiles, bands, patches, pair_patch, pair_atm, numerators, counts):
@@ -553,13 +561,15 @@
             in_specs=[smem, smem, anywhere, anywhere, anywhere],
             out_specs=vmem,
             scratch_shapes=[
-                pltpu.VMEM(recv_shape.shape, jnp.float32),
+                pltpu.VMEM((4 * reach * bucket,) + block, jnp.float32),
                 pltpu.VMEM(beside_shape.shape, jnp.float32),
                 pltpu.VMEM((bucket,) + block, jnp.float32),
-                pltpu.SemaphoreType.DMA((2 * reach + 2,)),
+                pltpu.SMEM((4 * reach * bucket + 1,), jnp.int32),
+                pltpu.SMEM((4 * reach * bucket + 1,), jnp.int32),
+                pltpu.SemaphoreType.DMA((3,)),
             ],
             name="take",
-        )(labels, table, send, recv, beside)
+        )(labels, table, send, recv.reshape((4 * reach * bucket,) + block), beside)
         return out.reshape(blocks_owned * cell_rows, flux)
 
     def padded(patches, pair_patch, pair_atm, numerators, counts, labels, table, send, recv, beside):

time: 53 us -> 51.9 us (0.979)
  Pallas kernels: 49.1 us -> 48.4 us
    pallas_call x1, Pallas kernels: 38.8 us -> 40.1 us  [adaptive(): pl.pallas_call(functools.partial(ring_kernel, tiles, bands, bucket), out_...]
    pallas_call x1, Pallas kernels: 4.51 us -> 3.17 us  [take(): pl.pallas_call(functools.partial(take_kernel, tiles, bands, bucket, block...]
    pallas_call x1, Pallas kernels: 5.81 us -> 5.1 us  [adaptive(): pl.pallas_call(functools.partial(list_kernel, tiles, bands, bucket, block...]
where the time goes in v4:
time: 51.9 us
  Pallas kernels  48.4 us (93%)
  between operations  1.38 us (3%)
  local copies, waits for them, and re-layouts  1.33 us (3%)
  other arithmetic  0.74 us (1%)
    pallas_call x1, Pallas kernels, adaptive(): pl.pallas_call(functools.partial(ring_kernel, tiles, bands, bucket), out_...  40.1 us
    pallas_call x1, Pallas kernels, adaptive(): pl.pallas_call(functools.partial(list_kernel, tiles, bands, bucket, block...  5.1 us
    pallas_call x1, Pallas kernels, take(): pl.pallas_call(functools.partial(take_kernel, tiles, bands, bucket, block...  3.17 us
    unnamed x8, local copies, waits for them, and re-layouts  1.33 us

profile of v4, /device:TPU:0, one launch (start us, length us, event | category | flops | bytes accessed | tf_op | source)
XLA Modules:
  0.0 51.9 jit_solution(5686616397526160492)
XLA Ops:
  0.7 0.0 copy-start
  0.7 0.0 copy-start.2
  0.7 0.0 copy-start.3
  0.7 5.1 %list.1 = (f32[81,32,128]{2,1,0:T(8,128)S(1)}, s32[1,128]{1,0:T(1,128)S(1)}) custom-call(s32[128]{0:T(128)} %patch_ref.1, s32[128]{0:T(128)} %atm_ref.1, s32[1]{0:T(128)S(6)} %copy.10.counts_ref, bf16[8192,128]{1,0:T(8,128)(2,1)} %patches_hbm.1, s32[128,32,128]{2,1,0:T(8,128)} %bitcast.5), custom_call_target="tpu_custom_call" | custom-call | tf_op jit(solution)/shard_map/list/pallas_call | solution.py:523
  5.8 40.1 %ring.1 = (f32[2,4,32,32,128]{4,3,2,1,0:T(8,128)}, f32[2,16,32,128]{3,2,1,0:T(8,128)}, s32[4,8,1,128]{3,2,1,0:T(1,128)S(1)}) custom-call(f32[81,32,128]{2,1,0:T(8,128)S(1)} %get-tuple-element.47.send_ref, s32[1,128]{1,0:T(1,128)S(1)} %get-tuple-element.48.labels_ref), custom_call_target="tpu_custom_call" | custom-call | tf_op jit(solution)/shard_map/ring/pallas_call | solution.py:539
  45.9 0.7 %slice_reduce_fusion = s32[]{:T(128)} fusion(s32[4,8,1,128]{3,2,1,0:T(1,128)S(1)} %get-tuple-element.49), kind=kLoop, calls=%fused_computation | loop fusion | flops 31 | bytes 132 | tf_op jit(solution)/shard_map/reduce_max | solution.py:578
  47.3 0.0 copy-done
  47.3 0.0 copy-done.2
  47.3 0.0 copy-done.3
  47.3 3.2 %conditional.1 = (f32[4096,128]{1,0:T(8,128)S(1)}) conditional(s32[]{:T(128)} %convert_element_type.3, (f32[2,4,32,32,128]{4,3,2,1,0:T(8,128)}, s32[1,128]{1,0:T(1,128)S(1)}, s32[4,8,1,128]{3,2,1,0:T(1,128)S(1)}, f32[81,32,128]{2,1,0:T(8,128)S(1)}, f32[2,16,32,128]{3,2,1,0:T(8,128)}) %tuple.11, (s32[128,128,32]{1,2,0:T(8,128)}, s32[128]{0:T(128)S(1)}, ...), branch_computations={%region_1.0_spmd, %region_2.0_spmd} | conditional | bytes 8 | solution.py:579
  47.4 3.2 %take.1 = f32[128,32,128]{2,1,0:T(8,128)S(1)} custom-call(s32[1,128]{1,0:T(1,128)S(1)} %get-tuple-element.28.labels_ref, s32[4,8,1,128]{3,2,1,0:T(1,128)S(1)} %get-tuple-element.29.table_ref, f32[81,32,128]{2,1,0:T(8,128)S(1)} %get-tuple-element.30.send_hbm, f32[256,32,128]{2,1,0:T(8,128)} %bitcast.7, f32[2,16,32,128]{3,2,1,0:T(8,128)} %get-tuple-element.32.beside_hbm), custom_call_target="tpu_custom_call" | custom-call | tf_op jit(solution)/shard_map/cond/branch_0_fun/take/pallas_call | solution.py:558
  50.5 0.0 copy-start.1
  50.6 1.3 %copy-done.1 = f32[4096,128]{1,0:T(8,128)} copy-done((f32[4096,128]{1,0:T(8,128)}, f32[4096,128]{1,0:T(8,128)S(1)}, u32[]{:S(2)}) %copy-start.1) | copy-done | bytes 2097176
Async XLA Ops:
  0.7 46.7 %copy-start = (bf16[8192,128]{1,0:T(8,128)(2,1)S(1)}, bf16[8192,128]{1,0:T(8,128)(2,1)}, u32[]{:S(2)}) copy-start(bf16[8192,128]{1,0:T(8,128)(2,1)} %patches_hbm.1) | copy-start | bytes 6291460
  0.7 46.7 %copy-start.2 = (s32[128]{0:T(128)S(1)}, s32[128]{0:T(128)}, u32[]{:S(2)}) copy-start(s32[128]{0:T(128)} %patch_ref.1) | copy-start | bytes 1540
  0.7 46.7 %copy-start.3 = (s32[128]{0:T(128)S(1)}, s32[128]{0:T(128)}, u32[]{:S(2)}) copy-start(s32[128]{0:T(128)} %atm_ref.1) | copy-start | bytes 1540
  50.5 1.3 %copy-start.1 = (f32[4096,128]{1,0:T(8,128)}, f32[4096,128]{1,0:T(8,128)S(1)}, u32[]{:S(2)}) copy-start(f32[4096,128]{1,0:T(8,128)S(1)} %get-tuple-element.55) | copy-start | bytes 6291460
